TPU v7x, 256 devices: a whole 4x4x8 slice. The times are simulated.
256 devices in a mesh: seq: 32 (over y, x, core), vocab: 8 (over z).
Axes of the slice: x: 4, y: 4, z: 8, core: 2. Of those that a mesh axis runs over, the one named last changes fastest.
Arguments:
- hidden: bfloat16 [4096, 8192], P('seq'), may hold values from -120 to 120
- head: bfloat16 [8192, 65536], P(None, ('seq', 'vocab')), may hold values from -0.5 to 0.5
- mask: int32 [4096], P('seq'), may hold values from 0 to 1, as said below
Outputs:
- positionwise_uncertainty: float32 [4096], P('seq')
- average_uncertainty_reward: float32 [], replicated
- derivative_wrt_latent_vectors: bfloat16 [4096, 8192], P('seq', 'vocab')
Inputs may be any that keep to these rules, and one draw needn't show every extreme that they name: Among the 128 tokens of one index of seq at least half of 16 and at most 16 have mask 1, and the last index of seq has exactly 16; later indices have no fewer than earlier ones.
All inputs are finite; a program needn't handle non-finite values.
Results may differ from a plain program's by a relative error of at most 0.019.
Values may be sent and summed in bfloat16 or wider, within the bound.
A program may use at most 64 MiB of HBM per device.

v0:
```python
import jax
import jax.numpy as jnp
from jax import lax
from jax.sharding import Mesh
from jax.sharding import PartitionSpec as P

ACT_DEV = 16
SEQ = ("seq_0", "seq_1", "seq_2")
SEQ_VOCAB = ("seq_0", "seq_1", "seq_2", "vocab")


def gathered_once(array, axis):
    leaves = jax.tree.leaves(array)
    sequence = sorted(range(len(leaves)), key=lambda k: -leaves[k].size)
    width = (1, *leaves[sequence[0]].shape)[-1]
    lines = [
        jnp.pad(leaves[k].reshape(-1), (0, -leaves[k].size % width)).reshape(-1, width)
        for k in sequence
    ]
    both, at, found = (lax.all_gather(jnp.concatenate(lines), axis), 0, {})
    for k, line in zip(sequence, lines):
        slab = both[:, at : at + len(line)].reshape(len(both), -1)
        found[k] = slab[:, : leaves[k].size].reshape(-1, *leaves[k].shape)
        at += len(line)
    numbers = iter(range(len(leaves)))
    return jax.tree.map(lambda _: found[next(numbers)], array)


def combined_by_axis(array, axes, combine):
    for axis in axes:
        pieces = gathered_once(array, axis)
        array = jax.tree.map(lambda part: part[0], pieces)
        for k in range(1, lax.axis_size(axis)):
            array = combine(array, jax.tree.map(lambda part: part[k], pieces))
    return array


def cut_along(array, dim, devices):
    before, after = (array.shape[:dim], array.shape[dim + 1 :])
    return jnp.moveaxis(array.reshape(*before, devices, -1, *after), dim, 0)


def sent_and_summed(array, axis, dim):
    pieces = cut_along(array, dim, lax.axis_size(axis))
    arrived = lax.all_to_all(pieces, axis, split_axis=0, concat_axis=0, tiled=True)
    return arrived.astype(jnp.float32).sum(axis=0)


def from_everyone(array, axis):
    devices = lax.axis_size(axis)
    return lax.all_to_all(
        jnp.broadcast_to(array[None], (devices, *array.shape)), axis, 0, 0, tiled=True
    )


def taken_together(array, axis):
    return from_everyone(array, axis).sum(axis=0)


def packed_total(arrays, axis):
    ends = [0]
    for a in arrays:
        ends.append(ends[-1] + a.size)
    total = taken_together(jnp.concatenate([a.ravel() for a in arrays]), axis)
    return tuple((total[b:e].reshape(a.shape) for a, b, e in zip(arrays, ends, ends[1:])))


def combine_rows(first, second):
    top = jnp.maximum(first[0], second[0])
    left = jnp.exp(first[0] - top)
    right = jnp.exp(second[0] - top)
    return (top, first[1] * left + second[1] * right, first[2] * left + second[2] * right)


def body(hidden, head, mask):
    inclusion_indicator = mask.astype(jnp.float32)
    slots = jnp.cumsum(mask) - 1
    picker = (slots[None, :] == jnp.arange(ACT_DEV, dtype=jnp.int32)[:, None]) & (
        mask[None, :] == 1
    )
    picker = picker.astype(jnp.bfloat16)
    source = jnp.dot(picker, hidden, preferred_element_type=jnp.float32).astype(jnp.bfloat16)
    rows_here = source.shape[0]
    logits = jnp.dot(
        lax.all_gather(source, SEQ, axis=0, tiled=True), head, preferred_element_type=jnp.float32
    )
    local_top = jnp.max(logits, axis=1)
    local_ex = jnp.exp(logits - local_top[:, None])
    top, total, weighted = combined_by_axis(
        (local_top, jnp.sum(local_ex, axis=1), jnp.sum(local_ex * logits, axis=1)),
        SEQ_VOCAB,
        combine_rows,
    )
    ex = jnp.exp(logits - top[:, None])
    mean_logit = weighted / total
    distribution_uncertainty = top + jnp.log(total) - mean_logit
    prob = ex / total[:, None]
    score_grad = (-(prob * (logits - mean_logit[:, None]))).astype(jnp.bfloat16)
    partial_grad = lax.psum_scatter(
        lax.dot_general(
            score_grad, head, (((1,), (1,)), ((), ())), preferred_element_type=jnp.float32
        ).astype(jnp.bfloat16),
        SEQ,
        scatter_dimension=0,
        tiled=True,
    )
    column_grad = sent_and_summed(partial_grad, "vocab", 1)
    position = lax.axis_index(SEQ) * rows_here
    mine = lax.dynamic_slice_in_dim(distribution_uncertainty, position, rows_here, 0)
    spread = picker.astype(jnp.float32)
    mine = lax.dot_general(
        spread, mine[:, None], (((0,), (0,)), ((), ())), precision=lax.Precision.HIGHEST
    )[:, 0]
    column_grad = lax.dot_general(
        spread, column_grad, (((0,), (0,)), ((), ())), precision=lax.Precision.HIGHEST
    )
    positionwise_uncertainty = inclusion_indicator * mine
    aggregate_uncertainty, response_length_total = packed_total(
        (jnp.sum(positionwise_uncertainty), jnp.sum(inclusion_indicator)), SEQ
    )
    average_uncertainty_reward = aggregate_uncertainty / response_length_total
    derivative_wrt_latent_vectors = (inclusion_indicator[:, None] * column_grad).astype(
        jnp.bfloat16
    )
    return (positionwise_uncertainty, average_uncertainty_reward, derivative_wrt_latent_vectors)


def solution(mesh):
    finer = Mesh(
        mesh.devices.reshape(4, 4, 2, mesh.shape["vocab"]), ("seq_0", "seq_1", "seq_2", "vocab")
    )
    placed = (P(SEQ, None), P(None, SEQ_VOCAB), P(SEQ))
    return jax.shard_map(
        body, mesh=finer, in_specs=placed, out_specs=(P(SEQ), P(), P(SEQ, "vocab")), check_vma=False
    )
```

profile of v0, /device:TPU:2, one launch (start us, length us, event | category | flops | bytes accessed | tf_op | source)
XLA Modules:
  0.0 263.5 jit_solution(15623832513023680919)
XLA Ops:
  7.2 0.0 copy-start
  7.2 0.0 all-gather.10.cloned.1.call-start
  7.2 0.8 broadcast_compare_fusion
  8.0 0.8 copy.12
  8.8 0.2 reduce-window.8
  9.0 0.1 add_reduce_fusion
  9.1 1.1 convolution_convert_fusion.1
  10.2 0.0 all-gather.10.cloned.1.call-update
  10.2 0.0 reduce-scatter.2.cloned.1.call-start
  10.2 61.6 %all-gather.10.cloned.1.call-done = bf16[512,8192]{1,0:T(8,128)(2,1)} async-done(((bf16[16,8192]{1,0:T(8,128)(2,1)}), bf16[512,8192]{1,0:T(8,128)(2,1)}) %all-gather.10.cloned.1.call-update) | async-done | bytes 8388624 | tf_op jit(solution)/shard_map/all_gather | solution.py:85
  71.9 7.1 %fusion.72 = (f32[512]{0:T(512)S(1)}, f32[512,256]{0,1:T(8,128)S(1)}) fusion(bf16[512,8192]{1,0:T(8,128)(2,1)} %all-gather.10.cloned.1.call-done, bf16[8192,256]{1,0:T(8,128)(2,1)} %param.4), kind=kOutput, calls=%fused_computation.146 | convolution fusion | flops 2147614208 | bytes 13109248 | tf_op jit(solution)/shard_map/dot_general | solution.py:84
  79.0 0.1 fusion.2
  79.2 11.9 %all-gather.4 = f32[4,3,512]{2,1,0:T(4,128)S(1)} all-gather(f32[1,3,512]{2,1,0:T(4,128)S(1)} %maximum_bitcast_fusion), channel_id=2, replica_groups=mesh['seq_0'=4,'seq_1'=4,'seq_2'=2,'vocab'=8] {'seq_0'}, dimensions={0}, use_global_device_ids=true | all-gather | bytes 30720 | tf_op jit(solution)/shard_map/all_gather | solution.py:20
  91.2 11.9 %all-gather.5 = f32[4,3,512]{2,1,0:T(4,128)S(1)} all-gather(f32[1,3,512]{2,1,0:T(4,128)S(1)} %maximum_bitcast_fusion.1), channel_id=3, replica_groups=mesh['seq_0'=4,'seq_1'=4,'seq_2'=2,'vocab'=8] {'seq_1'}, dimensions={0}, use_global_device_ids=true | all-gather | bytes 30720 | tf_op jit(solution)/shard_map/all_gather | solution.py:20
  103.2 1.8 all-gather.6
  105.1 26.0 %all-gather.7 = f32[8,3,512]{2,1,0:T(4,128)S(1)} all-gather(f32[1,3,512]{2,1,0:T(4,128)S(1)} %maximum_bitcast_fusion.3), channel_id=5, replica_groups=mesh['seq_0'=4,'seq_1'=4,'seq_2'=2,'vocab'=8] {'vocab'}, dimensions={0}, use_global_device_ids=true | all-gather | bytes 55296 | tf_op jit(solution)/shard_map/all_gather | solution.py:20
  131.2 0.1 add_subtract_fusion
  131.3 5.6 %convolution_convert_fusion = bf16[512,8192]{1,0:T(8,128)(2,1)} fusion(bf16[8192,256]{1,0:T(8,128)(2,1)S(1)} %copy-done.1, f32[512,256]{0,1:T(8,128)S(1)} %get-tuple-element.48, f32[512]{0:T(512)S(1)} %get-tuple-element.6, f32[512]{0:T(512)S(1)} %get-tuple-element.7, f32[512]{0:T(512)S(1)} %get-tuple-element.8), kind=kOutput, calls=%fused_computation | convolution fusion | flops 2152464384 | bytes 13113344 | tf_op jit(solution)/shard_map/dot_general | solution.py:100
  136.9 0.0 reduce-scatter.2.cloned.1.call-update
  136.9 0.6 copy-done.2
  137.6 0.6 convert_reduce_fusion.1
  138.2 1.3 fusion.73
  139.5 1.4 pad_maximum_fusion
  140.8 0.6 broadcast_in_dim.2
  141.4 5.6 %all-to-all-start = ((f32[32,1,2]{2,1,0:T(1,128)}), f32[32,1,2]{2,1,0:T(1,128)S(1)}, u32[]{:S(2)}, u32[]{:S(2)}) async-start(f32[32,1,2]{2,1,0:T(1,128)} %broadcast_in_dim.2), calls=%async_computation | async-start | bytes 32768 | tf_op jit(solution)/shard_map/all_to_all | solution.py:51
  147.0 88.1 %reduce-scatter.2.cloned.1.call-done = bf16[16,8192]{1,0:T(8,128)(2,1)} async-done(((bf16[512,8192]{1,0:T(8,128)(2,1)}), bf16[16,8192]{1,0:T(8,128)(2,1)}) %reduce-scatter.2.cloned.1.call-update) | async-done | bytes 262160 | tf_op jit(solution)/shard_map/reduce_scatter | solution.py:99
  235.2 1.7 copy.20
  236.8 7.0 %all-to-all-start.1 = ((bf16[8,16,1024]{2,1,0:T(8,128)(2,1)}), bf16[8,16,1024]{2,1,0:T(8,128)(2,1)S(1)}, u32[]{:S(2)}, u32[]{:S(2)}) async-start(bf16[8,16,1024]{2,1,0:T(8,128)(2,1)} %bitcast.357), calls=%async_computation.2 | async-start | bytes 524288 | tf_op jit(solution)/shard_map/all_to_all | solution.py:45
  243.9 0.1 reduce_sum.58
  243.9 0.6 fusion.71
  245.9 8.4 %all-to-all-done.1 = bf16[8,16,1024]{2,1,0:T(8,128)(2,1)S(1)} async-done(((bf16[8,16,1024]{2,1,0:T(8,128)(2,1)}), bf16[8,16,1024]{2,1,0:T(8,128)(2,1)S(1)}, u32[]{:S(2)}, u32[]{:S(2)}) %all-to-all-start.1) | async-done | bytes 262176 | tf_op jit(solution)/shard_map/all_to_all | solution.py:45
  254.4 1.1 fusion
  (20 shorter events, 0.3 us)
Async XLA Ops:
  7.2 1.9 copy-start
  7.2 64.7 %all-gather.10.cloned.1.call-start = ((), (), s32[]{:S(2)}) async-start(), calls=%async_computation.3 | async-start | bytes 8650752 | tf_op jit(solution)/shard_map/all_gather | solution.py:85
  10.2 225.0 %reduce-scatter.2.cloned.1.call-start = ((), (), s32[]{:S(2)}) async-start(), calls=%async_computation.4 | async-start | bytes 8650752 | tf_op jit(solution)/shard_map/reduce_scatter | solution.py:99
  71.9 59.4 %copy-start.1 = (bf16[8192,256]{1,0:T(8,128)(2,1)S(1)}, bf16[8192,256]{1,0:T(8,128)(2,1)}, u32[]{:S(2)}) copy-start(bf16[8192,256]{1,0:T(8,128)(2,1)} %param.4) | copy-start | bytes 12582916
  136.9 0.7 copy-start.2
  141.4 95.4 %all-to-all-start = ((f32[32,1,2]{2,1,0:T(1,128)}), f32[32,1,2]{2,1,0:T(1,128)S(1)}, u32[]{:S(2)}, u32[]{:S(2)}) async-start(f32[32,1,2]{2,1,0:T(1,128)} %broadcast_in_dim.2), calls=%async_computation | async-start | bytes 32768 | tf_op jit(solution)/shard_map/all_to_all | solution.py:51
  236.8 17.5 %all-to-all-start.1 = ((bf16[8,16,1024]{2,1,0:T(8,128)(2,1)}), bf16[8,16,1024]{2,1,0:T(8,128)(2,1)S(1)}, u32[]{:S(2)}, u32[]{:S(2)}) async-start(bf16[8,16,1024]{2,1,0:T(8,128)(2,1)} %bitcast.357), calls=%async_computation.2 | async-start | bytes 524288 | tf_op jit(solution)/shard_map/all_to_all | solution.py:45
Sparse Core Ops, SparseCore 0:
  11.1 60.7 all-gather.9
  137.0 98.0 reduce-scatter.1
where the time goes:
time: 264 us; the launch traced here: 263 us
  waiting for transfers between devices  158 us (60%)
  blocking collectives  51.7 us (20%)
  between operations  16.7 us (6%)
  matrix products  16.3 us (6%)
  starting transfers between devices  12.7 us (5%)
  local copies, waits for them, and re-layouts  4.31 us (2%)
  other arithmetic  3.53 us (1%)
    reduce_scatter x1, waiting for transfers between devices, body(): lax.psum_scatter(lax.dot_general(score_grad, head, (((1,), (1,)), ((), ()...  88.1 us
    all_gather x1, waiting for transfers between devices, body(): lax.all_gather(source, SEQ, axis=0, tiled=True)  61.6 us
    all_gather x4, blocking collectives, gathered_once(): both, at, found = (lax.all_gather(jnp.concatenate(lines), axis), 0, {})  51.7 us
    all_to_all x1, waiting for transfers between devices, sent_and_summed(): lax.all_to_all(pieces, axis, split_axis=0, concat_axis=0, tiled=True)  8.45 us
    dot_general x1, matrix products, body(): jnp.dot(lax.all_gather(source, SEQ, axis=0, tiled=True), head, preferred_...  7.11 us
    all_to_all x1, starting transfers between devices, sent_and_summed(): lax.all_to_all(pieces, axis, split_axis=0, concat_axis=0, tiled=True)  7.02 us
    dot_general x1, matrix products, body(): lax.dot_general(score_grad, head, (((1,), (1,)), ((), ())), preferred_ele...  5.64 us
    all_to_all x1, starting transfers between devices, from_everyone(): lax.all_to_all(jnp.broadcast_to(array[None], (devices, *array.shape)), ax...  5.56 us
  transfers between devices with their start and end apart: 4, of which 3 were waited for; matrix products, arithmetic and copies ran while one was open for 2% of the time, Pallas kernels for 0%

commit v1 on v0

--- a/solution.py
+++ b/solution.py
@@ -82,7 +82,11 @@
     source = jnp.dot(picker, hidden, preferred_element_type=jnp.float32).astype(jnp.bfloat16)
     rows_here = source.shape[0]
     logits = jnp.dot(
-        lax.all_gather(source, SEQ, axis=0, tiled=True), head, preferred_element_type=jnp.float32
+        jnp.concatenate(
+            lax.all_to_all(jnp.stack([source] * lax.axis_size(SEQ)), SEQ, 0, 0), axis=0
+        ),
+        head,
+        preferred_element_type=jnp.float32,
     )
     local_top = jnp.max(logits, axis=1)
     local_ex = jnp.exp(logits - local_top[:, None])

time: 264 us -> 305 us (1.16)
  blocking collectives: 51.7 us -> 155 us
  waiting for transfers between devices: 158 us -> 95.9 us
    all_to_all x0 -> x1, blocking collectives: none -> 102 us  [body(): lax.all_to_all(jnp.stack([source] * lax.axis_size(SEQ)), SEQ, 0, 0)]
    all_gather x1 -> x0, waiting for transfers between devices: 61.6 us -> none  [body(): lax.all_gather(source, SEQ, axis=0, tiled=True)]
  transfers between devices with their start and end apart: 4 -> 3, of which waited for: 3 -> 2; matrix products, arithmetic and copies ran while one was open for 2% -> 2% of each run, Pallas kernels for 0% -> 0%
where the time goes in v1:
time: 305 us
  blocking collectives  155 us (51%)
  waiting for transfers between devices  95.9 us (31%)
  between operations  16.7 us (5%)
  matrix products  15.3 us (5%)
  starting transfers between devices  13.5 us (4%)
  local copies, waits for them, and re-layouts  5.31 us (2%)
  other arithmetic  3.53 us (1%)
    all_to_all x1, blocking collectives, body(): lax.all_to_all(jnp.stack([source] * lax.axis_size(SEQ)), SEQ, 0, 0)  102 us
    reduce_scatter x1, waiting for transfers between devices, body(): lax.psum_scatter(lax.dot_general(score_grad, head, (((1,), (1,)), ((), ()...  87.4 us
    all_gather x4, blocking collectives, gathered_once(): both, at, found = (lax.all_gather(jnp.concatenate(lines), axis), 0, {})  52.7 us
    all_to_all x1, waiting for transfers between devices, sent_and_summed(): lax.all_to_all(pieces, axis, split_axis=0, concat_axis=0, tiled=True)  8.45 us
    dot_general x1, matrix products, body(): lax.dot_general(score_grad, head, (((1,), (1,)), ((), ())), preferred_ele...  7.84 us
    all_to_all x1, starting transfers between devices, sent_and_summed(): lax.all_to_all(pieces, axis, split_axis=0, concat_axis=0, tiled=True)  7 us
    all_to_all x1, starting transfers between devices, from_everyone(): lax.all_to_all(jnp.broadcast_to(array[None], (devices, *array.shape)), ax...  6.45 us
  transfers between devices with their start and end apart: 3, of which 2 were waited for; matrix products, arithmetic and copies ran while one was open for 2% of the time, Pallas kernels for 0%

profile of v1, /device:TPU:2, one launch (start us, length us, event | category | flops | bytes accessed | tf_op | source)
XLA Modules:
  0.0 304.9 jit_solution(428424245421309867)
XLA Ops:
  7.2 0.0 copy-start
  7.2 0.0 reduce-scatter.2.cloned.1.call-start
  7.2 0.8 broadcast_compare_fusion
  8.0 0.8 copy.12
  8.8 0.2 reduce-window.8
  9.0 0.1 add_reduce_fusion
  9.1 0.4 convolution_convert_fusion.1
  9.5 1.0 stack.2
  10.5 102.1 %all_to_all.16 = bf16[32,16,8192]{2,1,0:T(8,128)(2,1)S(1)} all-to-all(bf16[32,16,8192]{2,1,0:T(8,128)(2,1)S(1)} %stack.2), channel_id=1, replica_groups=mesh['seq_0'=4,'seq_1'=4,'seq_2'=2,'vocab'=8] {'seq_0','seq_1','seq_2'}, dimensions={0} | all-to-all | bytes 16777216 | tf_op jit(solution)/shard_map/all_to_all | solution.py:86
  112.5 4.6 %fusion.72 = (f32[512]{0:T(512)S(1)}, f32[512,256]{0,1:T(8,128)S(1)}) fusion(bf16[512,8192]{1,0:T(8,128)(2,1)S(1)} %bitcast.359, bf16[8192,256]{1,0:T(8,128)(2,1)} %param.4), kind=kOutput, calls=%fused_computation.146 | convolution fusion | flops 2147614208 | bytes 13109248 | tf_op jit(solution)/shard_map/dot_general | solution.py:84
  117.2 0.1 fusion.2
  117.3 11.9 %all-gather.4 = f32[4,3,512]{2,1,0:T(4,128)S(1)} all-gather(f32[1,3,512]{2,1,0:T(4,128)S(1)} %maximum_bitcast_fusion), channel_id=2, replica_groups=mesh['seq_0'=4,'seq_1'=4,'seq_2'=2,'vocab'=8] {'seq_0'}, dimensions={0}, use_global_device_ids=true | all-gather | bytes 30720 | tf_op jit(solution)/shard_map/all_gather | solution.py:20
  129.3 10.7 %all-gather.5 = f32[4,3,512]{2,1,0:T(4,128)S(1)} all-gather(f32[1,3,512]{2,1,0:T(4,128)S(1)} %maximum_bitcast_fusion.1), channel_id=3, replica_groups=mesh['seq_0'=4,'seq_1'=4,'seq_2'=2,'vocab'=8] {'seq_1'}, dimensions={0}, use_global_device_ids=true | all-gather | bytes 30720 | tf_op jit(solution)/shard_map/all_gather | solution.py:20
  140.1 1.8 all-gather.6
  142.0 28.2 %all-gather.7 = f32[8,3,512]{2,1,0:T(4,128)S(1)} all-gather(f32[1,3,512]{2,1,0:T(4,128)S(1)} %maximum_bitcast_fusion.3), channel_id=5, replica_groups=mesh['seq_0'=4,'seq_1'=4,'seq_2'=2,'vocab'=8] {'vocab'}, dimensions={0}, use_global_device_ids=true | all-gather | bytes 55296 | tf_op jit(solution)/shard_map/all_gather | solution.py:20
  170.3 0.1 add_subtract_fusion
  170.4 7.8 %convolution_convert_fusion = bf16[512,8192]{1,0:T(8,128)(2,1)} fusion(bf16[8192,256]{1,0:T(8,128)(2,1)} %param.4, f32[512,256]{0,1:T(8,128)S(1)} %get-tuple-element.48, f32[512]{0:T(512)S(1)} %get-tuple-element.6, f32[512]{0:T(512)S(1)} %get-tuple-element.7, f32[512]{0:T(512)S(1)} %get-tuple-element.8), kind=kOutput, calls=%fused_computation | convolution fusion | flops 2152464384 | bytes 13113344 | tf_op jit(solution)/shard_map/dot_general | solution.py:104
  178.2 0.0 reduce-scatter.2.cloned.1.call-update
  178.2 0.6 copy-done.1
  178.9 0.6 convert_reduce_fusion.1
  179.5 1.3 fusion.73
  180.8 1.4 pad_maximum_fusion
  182.1 0.6 broadcast_in_dim.2
  182.7 6.4 %all-to-all-start.1 = ((f32[32,1,2]{2,1,0:T(1,128)}), f32[32,1,2]{2,1,0:T(1,128)S(1)}, u32[]{:S(2)}, u32[]{:S(2)}) async-start(f32[32,1,2]{2,1,0:T(1,128)} %broadcast_in_dim.2), calls=%async_computation.1 | async-start | bytes 32768 | tf_op jit(solution)/shard_map/all_to_all | solution.py:51
  189.2 87.4 %reduce-scatter.2.cloned.1.call-done = bf16[16,8192]{1,0:T(8,128)(2,1)} async-done(((bf16[512,8192]{1,0:T(8,128)(2,1)}), bf16[16,8192]{1,0:T(8,128)(2,1)}) %reduce-scatter.2.cloned.1.call-update) | async-done | bytes 262160 | tf_op jit(solution)/shard_map/reduce_scatter | solution.py:103
  276.6 1.7 copy.20
  278.3 0.0 all-to-all-done.1
  278.3 7.0 %all-to-all-start.2 = ((bf16[8,16,1024]{2,1,0:T(8,128)(2,1)}), bf16[8,16,1024]{2,1,0:T(8,128)(2,1)S(1)}, u32[]{:S(2)}, u32[]{:S(2)}) async-start(bf16[8,16,1024]{2,1,0:T(8,128)(2,1)} %bitcast.358), calls=%async_computation.3 | async-start | bytes 524288 | tf_op jit(solution)/shard_map/all_to_all | solution.py:45
  285.3 0.1 reduce_sum.58
  285.3 0.6 fusion.71
  287.3 8.4 %all-to-all-done.2 = bf16[8,16,1024]{2,1,0:T(8,128)(2,1)S(1)} async-done(((bf16[8,16,1024]{2,1,0:T(8,128)(2,1)}), bf16[8,16,1024]{2,1,0:T(8,128)(2,1)S(1)}, u32[]{:S(2)}, u32[]{:S(2)}) %all-to-all-start.2) | async-done | bytes 262176 | tf_op jit(solution)/shard_map/all_to_all | solution.py:45
  295.8 1.1 fusion
  (17 shorter events, 0.3 us)
Async XLA Ops:
  7.2 1.9 copy-start
  7.2 269.4 %reduce-scatter.2.cloned.1.call-start = ((), (), s32[]{:S(2)}) async-start(), calls=%async_computation.4 | async-start | bytes 8650752 | tf_op jit(solution)/shard_map/reduce_scatter | solution.py:103
  178.2 0.7 copy-start.1
  182.7 95.5 %all-to-all-start.1 = ((f32[32,1,2]{2,1,0:T(1,128)}), f32[32,1,2]{2,1,0:T(1,128)S(1)}, u32[]{:S(2)}, u32[]{:S(2)}) async-start(f32[32,1,2]{2,1,0:T(1,128)} %broadcast_in_dim.2), calls=%async_computation.1 | async-start | bytes 32768 | tf_op jit(solution)/shard_map/all_to_all | solution.py:51
  278.3 17.5 %all-to-all-start.2 = ((bf16[8,16,1024]{2,1,0:T(8,128)(2,1)}), bf16[8,16,1024]{2,1,0:T(8,128)(2,1)S(1)}, u32[]{:S(2)}, u32[]{:S(2)}) async-start(bf16[8,16,1024]{2,1,0:T(8,128)(2,1)} %bitcast.358), calls=%async_computation.3 | async-start | bytes 524288 | tf_op jit(solution)/shard_map/all_to_all | solution.py:45
Sparse Core Ops, SparseCore 0:
  178.3 98.2 reduce-scatter.1
